TPU v7x, 32 devices: a whole 2x2x4 slice. The times are simulated.
32 devices in a mesh: gz: 2 (over core), row: 4 (over y, x), col: 4 (over z).
Axes of the slice: x: 2, y: 2, z: 4, core: 2. Of those that a mesh axis runs over, the one named last changes fastest.
Arguments:
- right_sides: float32 [32, 4, 16, 256], P(('gz', 'row', 'col')), may hold values from -6 to 6
- lower_inverse: bfloat16 [32, 4, 256, 256], P(('gz', 'row', 'col')), may hold values from -0.375 to 0.375
- upper_inverse: bfloat16 [32, 4, 256, 256], P(('gz', 'row', 'col')), may hold values from -0.375 to 0.375
- lower_blocks: bfloat16 [32, 4, 2, 256, 256], P(('gz', 'row', 'col')), may hold values from -0.125 to 0.125
- upper_blocks: bfloat16 [32, 4, 2, 256, 256], P(('gz', 'row', 'col')), may hold values from -0.125 to 0.125
- node_widths: int32 [32, 4], P(('gz', 'row', 'col')), may hold values from 128 to 256, as said below
- far_levels: int32 [32, 4], P(('gz', 'row', 'col')), may hold values from 0 to 5, as said below
- owner_level: int32 [32], replicated, may hold values from 0 to 5, as said below
Outputs:
- solution: float32 [32, 4, 16, 256], P(('gz', 'row', 'col'))
Inputs may be any that keep to these rules, and one draw needn't show every extreme that they name: Columns c >= node_widths of a supernode are padding; every device holds a supernode with all 256 columns. `far_levels`: between 2 and 5 where the supernode has two or more ancestors, but never past the root; 1 where it has one; 0 for the root and for the slot of the device that owns no separator. `owner_level`: every separator of level u is owned by exactly one device of its group (the devices t with the same t // 2**u); one device owns none and holds 0.
All inputs are finite; a program needn't handle non-finite values.
Results may differ from a plain program's by a relative error of at most 0.018.
Values may be sent and summed in bfloat16 or wider, within the bound.
A program may use at most 64 MiB of HBM per device.

v0:
```python
import jax
import jax.numpy as jnp
from jax import lax
from jax.sharding import PartitionSpec as P

W = 256
RHS = 16
NB = 2
LOCAL_LEVELS = 2
LOCAL_COUNT = 3


def level_start(height):
    return 2**LOCAL_LEVELS - 2 ** (LOCAL_LEVELS - height)


def apply_blocks(vectors, blocks):
    return jnp.einsum("snrk,snak->snra", vectors, blocks, preferred_element_type=jnp.float32)


def apply_single(vectors, blocks):
    return jnp.einsum("srk,sak->sra", vectors, blocks, preferred_element_type=jnp.float32)


def forward_local(right_sides, lower_inverse, lower_blocks, padding, far_levels, upper_levels):
    batch_size = right_sides.shape[0]
    pending = jnp.zeros((batch_size, LOCAL_COUNT, RHS, W), jnp.float32)
    upper_pending = jnp.zeros((batch_size, upper_levels, RHS, W), jnp.float32)
    solved = []
    for height in range(LOCAL_LEVELS):
        offset = level_start(height)
        amount = 2 ** (LOCAL_LEVELS - 1 - height)
        residue = (
            right_sides[:, offset : offset + amount] - pending[:, offset : offset + amount]
        ).astype(jnp.bfloat16)
        solved_now = padding[:, offset : offset + amount] * apply_blocks(
            residue, lower_inverse[:, offset : offset + amount]
        )
        solved.append(solved_now)
        rounded = solved_now.astype(jnp.bfloat16)
        for block_id in range(NB):
            product = apply_blocks(rounded, lower_blocks[:, offset : offset + amount, block_id])
            for distance in range(1, upper_levels + 1):
                if block_id == 0 and distance > 1:
                    continue
                if block_id == 0:
                    chosen = product
                else:
                    matches = far_levels[:, offset : offset + amount] == distance
                    chosen = jnp.where(matches[:, :, None, None], product, 0.0)
                target = height + distance
                if target < LOCAL_LEVELS:
                    target_count = amount // 2**distance
                    folded = chosen.reshape(batch_size, target_count, 2**distance, RHS, W).sum(
                        axis=2
                    )
                    begin_at = level_start(target)
                    pending = pending.at[:, begin_at : begin_at + target_count].add(folded)
                else:
                    upper_pending = upper_pending.at[:, target - LOCAL_LEVELS].add(
                        chosen.sum(axis=1)
                    )
    return (jnp.concatenate(solved, axis=1), upper_pending)


def backward_local(forward, upper_inverse, upper_blocks, padding, far_levels, upper_known):
    upper_levels = upper_known.shape[1]
    solutions = [None] * LOCAL_LEVELS
    for height in reversed(range(LOCAL_LEVELS)):
        offset = level_start(height)
        amount = 2 ** (LOCAL_LEVELS - 1 - height)
        residue = forward[:, offset : offset + amount]
        for block_id in range(NB):
            operand = jnp.zeros(residue.shape, jnp.float32)
            for distance in range(1, upper_levels + 1):
                if block_id == 0 and distance > 1:
                    continue
                target = height + distance
                if target < LOCAL_LEVELS:
                    known_part = jnp.repeat(solutions[target], 2**distance, axis=1)
                else:
                    known_part = jnp.broadcast_to(
                        upper_known[:, target - LOCAL_LEVELS][:, None], residue.shape
                    )
                if block_id == 0:
                    operand = known_part
                else:
                    matches = far_levels[:, offset : offset + amount] == distance
                    operand = operand + jnp.where(matches[:, :, None, None], known_part, 0.0)
            residue = residue - apply_blocks(
                operand.astype(jnp.bfloat16), upper_blocks[:, offset : offset + amount, block_id]
            )
        solutions[height] = padding[:, offset : offset + amount] * apply_blocks(
            residue.astype(jnp.bfloat16), upper_inverse[:, offset : offset + amount]
        )
    return jnp.concatenate(solutions, axis=1)


def spread_slots(partial_value, slot_count, slot_at):
    chosen = (jnp.arange(slot_count, dtype=jnp.int32) == slot_at)[:, None, None]
    return jnp.where(chosen, partial_value, 0.0)


def group_total(partial_value, height, layout, places):
    col_levels, grid_levels, col_span, grid_span, total_span = layout
    if height <= col_levels:
        slot_at = places[0] // 2**height
        summed = lax.psum(
            spread_slots(partial_value, col_span // 2**height, slot_at).astype(jnp.bfloat16), "col"
        ).astype(jnp.float32)
    elif height <= grid_levels:
        slot_at = places[1] // 2**height
        summed = lax.psum(
            spread_slots(partial_value, grid_span // 2**height, slot_at), ("row", "col")
        )
    else:
        slot_at = places[2] // 2**height
        summed = lax.psum(
            spread_slots(partial_value, total_span // 2**height, slot_at), ("gz", "row", "col")
        )
    return lax.dynamic_index_in_dim(summed, slot_at, 0, keepdims=True)


def group_share(partial_value, height, layout, places):
    col_levels, grid_levels, col_span, grid_span, total_span = layout
    if height <= col_levels:
        slot_at = places[0] // 2**height
        summed = lax.psum(
            spread_slots(partial_value, col_span // 2**height, slot_at).astype(jnp.bfloat16), "col"
        ).astype(jnp.float32)
    elif height <= grid_levels:
        slot_at = places[1] // 2**height
        summed = lax.psum(
            spread_slots(partial_value, grid_span // 2**height, slot_at), ("row", "col")
        )
    else:
        slot_at = places[2] // 2**height
        summed = lax.psum(
            spread_slots(partial_value, total_span // 2**height, slot_at), ("gz", "row", "col")
        )
    return lax.dynamic_index_in_dim(summed, slot_at, 0, keepdims=True)


def local(
    right_sides,
    lower_inverse,
    upper_inverse,
    lower_blocks,
    upper_blocks,
    node_widths,
    far_levels,
    owner_level,
):
    col_span = lax.axis_size("col")
    row_span = lax.axis_size("row")
    layer_span = lax.axis_size("gz")
    col_levels = col_span.bit_length() - 1
    grid_levels = col_levels + row_span.bit_length() - 1
    upper_levels = grid_levels + layer_span.bit_length() - 1
    col_place = lax.axis_index("col")
    grid_place = lax.axis_index("row") * col_span + col_place
    device = lax.axis_index("gz") * row_span * col_span + grid_place
    layout = (
        col_levels,
        grid_levels,
        col_span,
        row_span * col_span,
        layer_span * row_span * col_span,
    )
    places = (col_place, grid_place, device)
    columns = jnp.arange(W, dtype=jnp.int32)
    padding = (columns[None, None, None, :] < node_widths[:, :, None, None]).astype(jnp.float32)
    forward_nodes, upper_pending = forward_local(
        right_sides[:, :LOCAL_COUNT],
        lower_inverse[:, :LOCAL_COUNT],
        lower_blocks[:, :LOCAL_COUNT],
        padding[:, :LOCAL_COUNT],
        far_levels[:, :LOCAL_COUNT],
        upper_levels,
    )
    own_rights = right_sides[:, LOCAL_COUNT]
    own_padding = padding[:, LOCAL_COUNT]
    own_far = far_levels[:, LOCAL_COUNT]
    my_level = lax.dynamic_index_in_dim(owner_level, device, 0, keepdims=False)
    own_forward = jnp.zeros((1, RHS, W), jnp.float32)
    for height in range(1, upper_levels + 1):
        gathered = group_total(upper_pending[:, height - 1], height, layout, places)
        owner_here = my_level == height
        residue = (own_rights - gathered).astype(jnp.bfloat16)
        solved_now = jnp.where(
            owner_here, own_padding * apply_single(residue, lower_inverse[:, LOCAL_COUNT]), 0.0
        )
        own_forward = own_forward + solved_now
        rounded = solved_now.astype(jnp.bfloat16)
        for block_id in range(NB):
            product = apply_single(rounded, lower_blocks[:, LOCAL_COUNT, block_id])
            for distance in range(1, upper_levels + 1):
                if block_id == 0 and distance > 1:
                    continue
                target = height + distance
                if target > upper_levels:
                    continue
                if block_id == 0:
                    chosen = product
                else:
                    chosen = jnp.where((own_far == distance)[:, None, None], product, 0.0)
                upper_pending = upper_pending.at[:, target - 1].add(chosen)
    upper_known = jnp.zeros((1, upper_levels, RHS, W), jnp.float32)
    own_solution = jnp.zeros((1, RHS, W), jnp.float32)
    for height in range(upper_levels, 0, -1):
        owner_here = my_level == height
        residue = own_forward
        for block_id in range(NB):
            operand = jnp.zeros((1, RHS, W), jnp.float32)
            for distance in range(1, upper_levels + 1):
                if block_id == 0 and distance > 1:
                    continue
                target = height + distance
                if target > upper_levels:
                    continue
                known_part = upper_known[:, target - 1]
                if block_id == 0:
                    operand = known_part
                else:
                    operand = operand + jnp.where(
                        (own_far == distance)[:, None, None], known_part, 0.0
                    )
            residue = residue - apply_single(
                operand.astype(jnp.bfloat16), upper_blocks[:, LOCAL_COUNT, block_id]
            )
        solved_now = jnp.where(
            owner_here,
            own_padding * apply_single(residue.astype(jnp.bfloat16), upper_inverse[:, LOCAL_COUNT]),
            0.0,
        )
        own_solution = own_solution + solved_now
        shared = group_share(solved_now, height, layout, places)
        upper_known = upper_known.at[:, height - 1].set(shared)
    local_solution = backward_local(
        forward_nodes,
        upper_inverse[:, :LOCAL_COUNT],
        upper_blocks[:, :LOCAL_COUNT],
        padding[:, :LOCAL_COUNT],
        far_levels[:, :LOCAL_COUNT],
        upper_known,
    )
    return jnp.concatenate([local_solution, own_solution[:, None]], axis=1)


def solution(mesh):
    return jax.shard_map(
        local,
        mesh=mesh,
        in_specs=(
            P(("gz", "row", "col"), None, None, None),
            P(("gz", "row", "col"), None, None, None),
            P(("gz", "row", "col"), None, None, None),
            P(("gz", "row", "col"), None, None, None, None),
            P(("gz", "row", "col"), None, None, None, None),
            P(("gz", "row", "col"), None),
            P(("gz", "row", "col"), None),
            P(),
        ),
        out_specs=P(("gz", "row", "col"), None, None, None),
        check_vma=False,
    )
```

profile of v0, /device:TPU:0, one launch (start us, length us, event | category | flops | bytes accessed | tf_op | source)
XLA Modules:
  0.0 453.6 jit_solution(13407759819667578866)
XLA Ops:
  0.0 0.0 copy-start.1
  0.0 0.7 compare_bitcast_fusion.3
  0.8 0.7 fusion.307
  1.5 1.1 convolution_multiply_fusion.1
  2.6 1.2 select_reduce_fusion.4
  3.9 0.0 copy-start.2
  3.9 1.4 convolution_multiply_fusion.13
  5.3 0.0 copy-done.1
  5.3 0.2 fusion.24
  5.5 0.0 copy-start.5
  5.5 0.7 copy-done.5
  6.1 0.6 fusion.324
  7.4 0.2 fusion.167
  10.1 0.0 copy-start.4
  10.1 0.1 select_convert_fusion.1
  10.2 20.5 %psum.70 = bf16[2,16,256]{2,1,0:T(8,128)(2,1)S(1)} all-reduce(bf16[2,16,256]{2,1,0:T(8,128)(2,1)S(1)} %select_convert_fusion.1), channel_id=1, replica_groups=mesh['gz'=2,'row'=4,'col'=4] {'col'}, use_global_device_ids=true, to_apply=%region_5.6 | all-reduce | flops 8192 | bytes 32768 | tf_op jit(solution)/shard_map/psum | solution.py:108
  30.7 0.0 copy-start.6
  30.7 0.7 copy-done.6
  31.4 0.6 dynamic_slice.24
  32.7 0.0 copy-done.2
  32.7 0.0 copy-done.4
  32.7 0.2 fusion.23
  32.8 0.2 fusion.22
  33.7 0.2 fusion.166
  35.9 8.5 %psum.71 = bf16[1,16,256]{2,1,0:T(8,128)(2,1)S(1)} all-reduce(bf16[1,16,256]{2,1,0:T(8,128)(2,1)S(1)} %fusion.218), channel_id=1, replica_groups=mesh['gz'=2,'row'=4,'col'=4] {'col'}, use_global_device_ids=true, to_apply=%region_6.7 | all-reduce | flops 4096 | bytes 16384 | tf_op jit(solution)/shard_map/psum | solution.py:108
  45.1 0.2 fusion.21
  45.2 0.2 fusion.20
  45.4 0.2 fusion.165
  45.7 0.1 broadcast_select_fusion.1
  45.8 75.8 %psum.72 = f32[2,16,256]{2,1,0:T(8,128)S(1)} all-reduce(f32[2,16,256]{2,1,0:T(8,128)S(1)} %broadcast_select_fusion.1), channel_id=1, replica_groups=mesh['gz'=2,'row'=4,'col'=4] {'row','col'}, use_global_device_ids=true, to_apply=%region_7.8 | all-reduce | flops 8192 | bytes 65536 | tf_op jit(solution)/shard_map/psum | solution.py:113
  122.3 0.2 fusion.19
  122.4 0.2 fusion.78
  122.6 0.2 fusion.18
  122.8 72.1 %psum.73 = f32[1,16,256]{2,1,0:T(8,128)S(1)} all-reduce(f32[1,16,256]{2,1,0:T(8,128)S(1)} %fusion.18), channel_id=1, replica_groups=mesh['gz'=2,'row'=4,'col'=4] {'row','col'}, use_global_device_ids=true, to_apply=%region_8.9 | all-reduce | flops 4096 | bytes 32768 | tf_op jit(solution)/shard_map/psum | solution.py:113
  195.5 0.0 copy-start.3
  195.5 0.2 fusion.14
  195.7 0.2 fusion.13
  195.9 0.2 fusion.12
  196.0 36.9 %psum.74 = f32[1,16,256]{2,1,0:T(8,128)S(1)} all-reduce(f32[1,16,256]{2,1,0:T(8,128)S(1)} %fusion.12), channel_id=1, replica_groups=mesh['gz'=2,'row'=4,'col'=4] {'gz','row','col'}, use_global_device_ids=true, to_apply=%region_9.10 | all-reduce | flops 4096 | bytes 32768 | tf_op jit(solution)/shard_map/psum | solution.py:118
  233.6 0.2 fusion.8
  233.7 0.0 copy-done
  233.7 0.2 convolution_subtract_fusion.13
  233.9 0.0 copy-done.3
  233.9 0.3 fusion.6
  234.3 41.4 %psum.75 = f32[1,16,256]{2,1,0:T(8,128)S(1)} all-reduce(f32[1,16,256]{2,1,0:T(8,128)S(1)} %select_bitcast_fusion.1), channel_id=1, replica_groups=mesh['gz'=2,'row'=4,'col'=4] {'gz','row','col'}, use_global_device_ids=true, to_apply=%region_10.11 | all-reduce | flops 4096 | bytes 32768 | tf_op jit(solution)/shard_map/psum | solution.py:138
  275.7 0.1 convolution_subtract_fusion.11
  275.9 0.3 fusion.5
  276.2 76.1 %psum.76 = f32[1,16,256]{2,1,0:T(8,128)S(1)} all-reduce(f32[1,16,256]{2,1,0:T(8,128)S(1)} %select_bitcast_fusion), channel_id=1, replica_groups=mesh['gz'=2,'row'=4,'col'=4] {'row','col'}, use_global_device_ids=true, to_apply=%region_11.12 | all-reduce | flops 4096 | bytes 32768 | tf_op jit(solution)/shard_map/psum | solution.py:133
  352.3 0.1 convolution_subtract_fusion.9
  352.5 0.3 fusion.4
  352.8 0.1 broadcast_select_fusion
  352.9 72.1 %psum.77 = f32[2,16,256]{2,1,0:T(8,128)S(1)} all-reduce(f32[2,16,256]{2,1,0:T(8,128)S(1)} %broadcast_select_fusion), channel_id=1, replica_groups=mesh['gz'=2,'row'=4,'col'=4] {'row','col'}, use_global_device_ids=true, to_apply=%region_12.13 | all-reduce | flops 8192 | bytes 65536 | tf_op jit(solution)/shard_map/psum | solution.py:133
  425.0 0.1 convolution_subtract_fusion.7
  425.1 0.3 fusion.3
  425.4 8.5 %psum.78 = bf16[1,16,256]{2,1,0:T(8,128)(2,1)S(1)} all-reduce(bf16[1,16,256]{2,1,0:T(8,128)(2,1)S(1)} %fusion.201), channel_id=1, replica_groups=mesh['gz'=2,'row'=4,'col'=4] {'col'}, use_global_device_ids=true, to_apply=%region_13.14 | all-reduce | flops 4096 | bytes 16384 | tf_op jit(solution)/shard_map/psum | solution.py:128
  434.0 0.2 convolution_subtract_fusion.5
  434.1 0.3 fusion.2
  434.4 0.1 select_convert_fusion
  434.5 17.4 %psum.79 = bf16[2,16,256]{2,1,0:T(8,128)(2,1)S(1)} all-reduce(bf16[2,16,256]{2,1,0:T(8,128)(2,1)S(1)} %select_convert_fusion), channel_id=1, replica_groups=mesh['gz'=2,'row'=4,'col'=4] {'col'}, use_global_device_ids=true, to_apply=%region_14.15 | all-reduce | flops 8192 | bytes 32768 | tf_op jit(solution)/shard_map/psum | solution.py:128
  451.9 0.2 convolution_subtract_fusion.3
  452.1 0.3 fusion.325
  452.4 0.2 convolution_subtract_fusion.1
  452.6 0.3 fusion
  453.0 0.6 pad_maximum_fusion
  (33 shorter events, 0.2 us)
Async XLA Ops:
  0.0 5.3 %copy-start.1 = (bf16[1,4,2,256,256]{4,3,2,1,0:T(8,128)(2,1)S(1)}, bf16[1,4,2,256,256]{4,3,2,1,0:T(8,128)(2,1)}, u32[]{:S(2)}) copy-start(bf16[1,4,2,256,256]{4,3,2,1,0:T(8,128)(2,1)} %param.73) | copy-start | bytes 3145732
  3.9 28.8 %copy-start.2 = (bf16[1,4,256,256]{3,2,1,0:T(8,128)(2,1)S(1)}, bf16[1,4,256,256]{3,2,1,0:T(8,128)(2,1)}, u32[]{:S(2)}) copy-start(bf16[1,4,256,256]{3,2,1,0:T(8,128)(2,1)} %param.71) | copy-start | bytes 1572868
  5.5 0.7 copy-start.5
  10.1 22.6 %copy-start.4 = (f32[1,4,16,256]{3,2,1,0:T(8,128)S(1)}, f32[1,4,16,256]{3,2,1,0:T(8,128)}, u32[]{:S(2)}) copy-start(f32[1,4,16,256]{3,2,1,0:T(8,128)} %param.70) | copy-start | bytes 196612
  30.7 0.7 copy-start.6
  45.4 188.3 %copy-start = (bf16[1,4,2,256,256]{4,3,2,1,0:T(8,128)(2,1)S(1)}, bf16[1,4,2,256,256]{4,3,2,1,0:T(8,128)(2,1)}, u32[]{:S(2)}) copy-start(bf16[1,4,2,256,256]{4,3,2,1,0:T(8,128)(2,1)} %param.74) | copy-start | bytes 3145732
  195.5 38.4 %copy-start.3 = (bf16[1,4,256,256]{3,2,1,0:T(8,128)(2,1)S(1)}, bf16[1,4,256,256]{3,2,1,0:T(8,128)(2,1)}, u32[]{:S(2)}) copy-start(bf16[1,4,256,256]{3,2,1,0:T(8,128)(2,1)} %param.72) | copy-start | bytes 1572868
where the time goes:
time: 454 us
  blocking collectives  429 us (94%)
  matrix products  9.61 us (2%)
  between operations  9.28 us (2%)
    psum x2, blocking collectives, group_share(): lax.psum(spread_slots(partial_value, grid_span // 2 ** height, slot_at),...  148 us
    psum x2, blocking collectives, group_total(): lax.psum(spread_slots(partial_value, grid_span // 2 ** height, slot_at),...  148 us
    psum x1, blocking collectives, group_share(): lax.psum(spread_slots(partial_value, total_span // 2 ** height, slot_at),...  41.4 us
    psum x1, blocking collectives, group_total(): lax.psum(spread_slots(partial_value, total_span // 2 ** height, slot_at),...  36.9 us
    psum x2, blocking collectives, group_total(): lax.psum(spread_slots(partial_value, col_span // 2 ** height, slot_at).as...  29 us
    psum x2, blocking collectives, group_share(): lax.psum(spread_slots(partial_value, col_span // 2 ** height, slot_at).as...  25.9 us

commit v1 on v0

--- a/solution.py
+++ b/solution.py
@@ -115,9 +115,9 @@
         )
     else:
         slot_at = places[2] // 2**height
-        summed = lax.psum(
-            spread_slots(partial_value, total_span // 2**height, slot_at), ("gz", "row", "col")
-        )
+        own = spread_slots(partial_value, total_span // 2**height, slot_at)
+        parts = lax.all_gather(own, ("gz", "row", "col"))
+        summed = jnp.sum(parts, axis=0)
     return lax.dynamic_index_in_dim(summed, slot_at, 0, keepdims=True)
 
 

time: 454 us -> 490 us (1.079)
  blocking collectives: 429 us -> 465 us
    all_gather x0 -> x1, blocking collectives: none -> 67.8 us  [group_total(): parts = lax.all_gather(own, ('gz', 'row', 'col'))]
    psum x1 -> x0, blocking collectives: 36.9 us -> none  [group_total(): lax.psum(spread_slots(partial_value, total_span // 2 ** height, slot_at),...]
where the time goes in v1:
time: 490 us
  blocking collectives  465 us (95%)
  matrix products  9.51 us (2%)
  between operations  9.24 us (2%)
    psum x2, blocking collectives, group_share(): lax.psum(spread_slots(partial_value, grid_span // 2 ** height, slot_at),...  149 us
    psum x2, blocking collectives, group_total(): lax.psum(spread_slots(partial_value, grid_span // 2 ** height, slot_at),...  148 us
    all_gather x1, blocking collectives, group_total(): parts = lax.all_gather(own, ('gz', 'row', 'col'))  67.8 us
    psum x1, blocking collectives, group_share(): lax.psum(spread_slots(partial_value, total_span // 2 ** height, slot_at),...  45.2 us
    psum x2, blocking collectives, group_total(): lax.psum(spread_slots(partial_value, col_span // 2 ** height, slot_at).as...  29 us
    psum x2, blocking collectives, group_share(): lax.psum(spread_slots(partial_value, col_span // 2 ** height, slot_at).as...  25.9 us

profile of v1, /device:TPU:0, one launch (start us, length us, event | category | flops | bytes accessed | tf_op | source)
XLA Modules:
  0.0 489.5 jit_solution(13581598720208869148)
XLA Ops:
  0.0 0.0 copy-start.1
  0.0 1.3 dynamic_slice.24
  4.6 1.4 fusion.323
  11.7 0.7 compare_bitcast_fusion.3
  12.3 0.7 fusion.306
  13.1 1.1 convolution_multiply_fusion.1
  14.2 1.2 select_reduce_fusion.4
  15.4 1.3 convolution_multiply_fusion.13
  16.7 0.0 copy-start.2
  16.8 0.0 copy-done.1
  16.8 0.2 fusion.23
  17.0 0.2 fusion.167
  17.2 0.0 copy-start.4
  17.3 0.1 select_convert_fusion.1
  17.3 20.5 %psum.63 = bf16[2,16,256]{2,1,0:T(8,128)(2,1)S(1)} all-reduce(bf16[2,16,256]{2,1,0:T(8,128)(2,1)S(1)} %select_convert_fusion.1), channel_id=1, replica_groups=mesh['gz'=2,'row'=4,'col'=4] {'col'}, use_global_device_ids=true, to_apply=%region_5.6 | all-reduce | flops 8192 | bytes 32768 | tf_op jit(solution)/shard_map/psum | solution.py:108
  37.9 0.0 copy-done.2
  37.9 0.0 copy-done.4
  37.9 0.2 fusion.22
  38.0 0.2 fusion.21
  38.2 0.2 fusion.166
  38.5 8.5 %psum.64 = bf16[1,16,256]{2,1,0:T(8,128)(2,1)S(1)} all-reduce(bf16[1,16,256]{2,1,0:T(8,128)(2,1)S(1)} %fusion.217), channel_id=1, replica_groups=mesh['gz'=2,'row'=4,'col'=4] {'col'}, use_global_device_ids=true, to_apply=%region_6.7 | all-reduce | flops 4096 | bytes 16384 | tf_op jit(solution)/shard_map/psum | solution.py:108
  47.0 0.2 fusion.20
  47.2 0.2 fusion.19
  47.4 0.2 fusion.165
  47.6 0.1 broadcast_select_fusion.1
  47.7 75.8 %psum.65 = f32[2,16,256]{2,1,0:T(8,128)S(1)} all-reduce(f32[2,16,256]{2,1,0:T(8,128)S(1)} %broadcast_select_fusion.1), channel_id=1, replica_groups=mesh['gz'=2,'row'=4,'col'=4] {'row','col'}, use_global_device_ids=true, to_apply=%region_7.8 | all-reduce | flops 8192 | bytes 65536 | tf_op jit(solution)/shard_map/psum | solution.py:113
  123.5 0.1 fusion.18
  123.7 0.2 fusion.77
  123.9 0.0 copy-start
  123.9 0.2 fusion.17
  124.1 72.2 %psum.66 = f32[1,16,256]{2,1,0:T(8,128)S(1)} all-reduce(f32[1,16,256]{2,1,0:T(8,128)S(1)} %fusion.17), channel_id=1, replica_groups=mesh['gz'=2,'row'=4,'col'=4] {'row','col'}, use_global_device_ids=true, to_apply=%region_8.9 | all-reduce | flops 4096 | bytes 32768 | tf_op jit(solution)/shard_map/psum | solution.py:113
  196.3 0.1 fusion.13
  196.4 0.2 fusion.12
  196.6 0.2 fusion.11
  196.8 67.8 %all_gather.4 = f32[32,1,16,256]{3,2,1,0:T(8,128)S(1)} all-gather(f32[1,1,16,256]{3,2,1,0:T(8,128)S(1)} %fusion.11), channel_id=1, replica_groups=mesh['gz'=2,'row'=4,'col'=4] {'gz','row','col'}, dimensions={0}, use_global_device_ids=true | all-gather | bytes 540672 | tf_op jit(solution)/shard_map/all_gather | solution.py:119
  264.6 0.0 copy-start.3
  264.6 0.2 fusion.8
  264.8 0.0 copy-done
  264.8 0.2 convolution_subtract_fusion.13
  265.0 0.7 copy-done.3
  265.6 0.3 fusion.6
  265.9 45.2 %psum.67 = f32[1,16,256]{2,1,0:T(8,128)S(1)} all-reduce(f32[1,16,256]{2,1,0:T(8,128)S(1)} %select_bitcast_fusion.1), channel_id=1, replica_groups=mesh['gz'=2,'row'=4,'col'=4] {'gz','row','col'}, use_global_device_ids=true, to_apply=%region_10.11 | all-reduce | flops 4096 | bytes 32768 | tf_op jit(solution)/shard_map/psum | solution.py:138
  311.1 0.1 convolution_subtract_fusion.11
  311.3 0.3 fusion.5
  311.6 76.6 %psum.68 = f32[1,16,256]{2,1,0:T(8,128)S(1)} all-reduce(f32[1,16,256]{2,1,0:T(8,128)S(1)} %select_bitcast_fusion), channel_id=1, replica_groups=mesh['gz'=2,'row'=4,'col'=4] {'row','col'}, use_global_device_ids=true, to_apply=%region_11.12 | all-reduce | flops 4096 | bytes 32768 | tf_op jit(solution)/shard_map/psum | solution.py:133
  388.2 0.1 convolution_subtract_fusion.9
  388.4 0.3 fusion.4
  388.7 0.1 broadcast_select_fusion
  388.8 72.1 %psum.69 = f32[2,16,256]{2,1,0:T(8,128)S(1)} all-reduce(f32[2,16,256]{2,1,0:T(8,128)S(1)} %broadcast_select_fusion), channel_id=1, replica_groups=mesh['gz'=2,'row'=4,'col'=4] {'row','col'}, use_global_device_ids=true, to_apply=%region_12.13 | all-reduce | flops 8192 | bytes 65536 | tf_op jit(solution)/shard_map/psum | solution.py:133
  460.9 0.1 convolution_subtract_fusion.7
  461.1 0.3 fusion.3
  461.4 8.5 %psum.70 = bf16[1,16,256]{2,1,0:T(8,128)(2,1)S(1)} all-reduce(bf16[1,16,256]{2,1,0:T(8,128)(2,1)S(1)} %fusion.200), channel_id=1, replica_groups=mesh['gz'=2,'row'=4,'col'=4] {'col'}, use_global_device_ids=true, to_apply=%region_13.14 | all-reduce | flops 4096 | bytes 16384 | tf_op jit(solution)/shard_map/psum | solution.py:128
  469.9 0.2 convolution_subtract_fusion.5
  470.1 0.3 fusion.2
  470.4 0.1 select_convert_fusion
  470.5 17.4 %psum.71 = bf16[2,16,256]{2,1,0:T(8,128)(2,1)S(1)} all-reduce(bf16[2,16,256]{2,1,0:T(8,128)(2,1)S(1)} %select_convert_fusion), channel_id=1, replica_groups=mesh['gz'=2,'row'=4,'col'=4] {'col'}, use_global_device_ids=true, to_apply=%region_14.15 | all-reduce | flops 8192 | bytes 32768 | tf_op jit(solution)/shard_map/psum | solution.py:128
  487.9 0.1 convolution_subtract_fusion.3
  488.0 0.3 fusion.324
  488.4 0.2 convolution_subtract_fusion.1
  488.6 0.3 fusion
  488.9 0.7 pad_maximum_fusion
  (33 shorter events, 0.3 us)
Async XLA Ops:
  0.0 16.8 %copy-start.1 = (bf16[1,4,2,256,256]{4,3,2,1,0:T(8,128)(2,1)S(1)}, bf16[1,4,2,256,256]{4,3,2,1,0:T(8,128)(2,1)}, u32[]{:S(2)}) copy-start(bf16[1,4,2,256,256]{4,3,2,1,0:T(8,128)(2,1)} %param.73) | copy-start | bytes 3145732
  16.7 21.1 %copy-start.2 = (bf16[1,4,256,256]{3,2,1,0:T(8,128)(2,1)S(1)}, bf16[1,4,256,256]{3,2,1,0:T(8,128)(2,1)}, u32[]{:S(2)}) copy-start(bf16[1,4,256,256]{3,2,1,0:T(8,128)(2,1)} %param.71) | copy-start | bytes 1572868
  17.2 20.6 %copy-start.4 = (f32[1,4,16,256]{3,2,1,0:T(8,128)S(1)}, f32[1,4,16,256]{3,2,1,0:T(8,128)}, u32[]{:S(2)}) copy-start(f32[1,4,16,256]{3,2,1,0:T(8,128)} %param.70) | copy-start | bytes 196612
  123.9 140.9 %copy-start = (bf16[1,4,2,256,256]{4,3,2,1,0:T(8,128)(2,1)S(1)}, bf16[1,4,2,256,256]{4,3,2,1,0:T(8,128)(2,1)}, u32[]{:S(2)}) copy-start(bf16[1,4,2,256,256]{4,3,2,1,0:T(8,128)(2,1)} %param.74) | copy-start | bytes 3145732
  264.6 1.0 copy-start.3
